TPU v7x, 256 devices: a whole 4x4x8 slice. The times are simulated.
256 devices in a mesh: blk: 16 (over z_hi, y, core), grid: 16 (over x, z_lo).
Axes of the slice: x: 4, y: 4, z: 8 (z_hi: 2, z_lo: 4; z = z_hi * 4 + z_lo), core: 2. Of those that a mesh axis runs over, the one named last changes fastest.
Arguments:
- constraints: float32 [131072, 1024], P(('blk', 'grid')), may hold values from -0.1875 to 0.1875
- times_x: float32 [131072, 1024], P(('blk', 'grid')), may hold values from -6 to 6
- times_zinv: float32 [131072, 1024], P(('blk', 'grid')), may hold values from -6 to 6
- owner: int32 [16, 16, 16], P('blk', 'grid'), may hold values from 0 to 15, each once within a row
- update: float32 [16, 16, 16, 32, 1024], P('blk', 'grid'), may hold values from -6 to 6
Outputs:
- owned: float32 [16, 16, 16, 32, 1024], P('blk', 'grid')
Inputs may be any that keep to these rules, and one draw needn't show every extreme that they name: Each owner[b, g, :] is a permutation of 0 to 15.
All inputs are finite; a program needn't handle non-finite values.
Results may differ from a plain program's by a relative error of at most 0.0003.
Values sent between devices are 32-bit elements; how exact they have to be, the bound alone decides.
A program may use at most 64 MiB of HBM per device.

v0:
```python
import jax
import jax.numpy as jnp
from jax import lax
from jax.sharding import PartitionSpec as P

ROUNDS = 2


def from_behind(array, axis, by):
    length = lax.axis_size(axis)
    return lax.ppermute(array, axis, [(i, (i + by) % length) for i in range(length)])


def hadamard_panel(rows_x, rows_z, panel):
    left = jnp.dot(
        rows_x, panel.T, preferred_element_type=jnp.float32, precision=lax.Precision.HIGHEST
    )
    right = jnp.dot(
        rows_z, panel.T, preferred_element_type=jnp.float32, precision=lax.Precision.HIGHEST
    )
    return left * right


def body(constraints, times_x, times_zinv, owner, update):
    groups = lax.axis_size("grid")
    row_count, width = times_x.shape
    tile_rows = row_count // groups
    places = jnp.arange(groups, dtype=jnp.int32)
    onehot = owner[0, 0][None, :] == places[:, None]
    inverse = jnp.sum(jnp.where(onehot, places[None, :], 0), axis=1)
    rows_x = times_x.reshape(groups, tile_rows, width)[inverse].reshape(row_count, width)
    rows_z = times_zinv.reshape(groups, tile_rows, width)[inverse].reshape(row_count, width)
    panel = constraints
    pieces = []
    for step in range(ROUNDS):
        if step > 0:
            panel = from_behind(panel, "blk", 1)
        block = hadamard_panel(rows_x, rows_z, panel).reshape(groups, tile_rows, panel.shape[0])
        pieces.append(block)
    joined = jnp.concatenate(pieces, axis=2)
    joined = lax.all_to_all(joined, "grid", split_axis=0, concat_axis=0, tiled=True)
    return joined[None, None] - update


def solution(mesh):
    placed = (
        P(("blk", "grid"), None),
        P(("blk", "grid"), None),
        P(("blk", "grid"), None),
        P("blk", "grid", None),
        P("blk", "grid", None, None, None),
    )
    return jax.shard_map(
        body,
        mesh=mesh,
        in_specs=placed,
        out_specs=P("blk", "grid", None, None, None),
        check_vma=False,
    )
```

profile of v0, /device:TPU:128, one launch (start us, length us, event | category | flops | bytes accessed | tf_op | source)
XLA Modules:
  0.0 112.6 jit_solution(16194590918542673646)
XLA Ops:
  0.0 0.0 copy-start
  0.0 0.0 collective-permute-start
  0.0 0.9 select_reduce_fusion
  0.9 0.7 copy-done
  1.6 2.0 %gather_fusion.1 = f32[16,32,1024]{2,1,0:T(8,128)} fusion(f32[16,32,1024]{2,1,0:T(8,128)S(1)} %bitcast.21, s32[1024]{0:T(1024)S(1)} %pad_clamp_fusion), kind=kCustom, calls=%fused_computation.1 | custom fusion | bytes 4194368 | tf_op jit(solution)/shard_map/gather | solution.py:32
  3.6 3.6 %gather_fusion = f32[16,32,1024]{2,1,0:T(8,128)} fusion(f32[16,32,1024]{2,1,0:T(8,128)} %bitcast.28, s32[1024]{0:T(1024)S(1)} %pad_clamp_fusion), kind=kCustom, calls=%fused_computation | custom fusion | bytes 4194368 | tf_op jit(solution)/shard_map/gather | solution.py:31
  7.2 0.0 copy-start.2
  7.2 0.0 copy-start.3
  7.2 5.9 %fusion.1 = f32[512,512]{1,0:T(8,128)S(1)} fusion(f32[512,1024]{1,0:T(8,128)} %bitcast.22, f32[512,1024]{1,0:T(8,128)} %param.5), kind=kOutput, calls=%fused_computation.11 | convolution fusion | flops 3221225472 | bytes 5242880 | tf_op jit(solution)/shard_map/dot_general | solution.py:15
  13.1 0.0 copy-done.2
  13.1 0.0 copy-done.3
  13.1 3.5 %convolution_multiply_fusion.1 = f32[512,512]{1,0:T(8,128)S(1)} fusion(f32[512,512]{1,0:T(8,128)S(1)} %fusion.1, f32[512,1024]{1,0:T(8,128)S(1)} %bitcast.24, f32[512,1024]{1,0:T(8,128)S(1)} %copy-done.3), kind=kOutput, calls=%fused_computation.5 | convolution fusion | flops 3221487616 | bytes 6291456 | tf_op jit(solution)/shard_map/dot_general | solution.py:18
  16.7 0.0 copy-start.1
  16.7 36.5 %collective-permute-done = f32[512,1024]{1,0:T(8,128)} collective-permute-done((f32[512,1024]{1,0:T(8,128)}, f32[512,1024]{1,0:T(8,128)}, u32[]{:S(2)}, u32[]{:S(2)}) %collective-permute-start) | collective-permute-done | bytes 2097184 | tf_op jit(solution)/shard_map/ppermute | solution.py:11
  53.2 5.1 %fusion.2 = f32[512,512]{1,0:T(8,128)S(1)} fusion(f32[512,1024]{1,0:T(8,128)S(1)} %bitcast.25, f32[512,1024]{1,0:T(8,128)} %collective-permute-done), kind=kOutput, calls=%fused_computation.12 | convolution fusion | flops 3221225472 | bytes 5242880 | tf_op jit(solution)/shard_map/dot_general | solution.py:18
  58.3 0.0 copy-done.1
  58.3 5.3 %convolution_multiply_fusion = f32[512,512]{1,0:T(8,128)S(1)} fusion(f32[512,512]{1,0:T(8,128)S(1)} %fusion.2, f32[512,1024]{1,0:T(8,128)S(1)} %bitcast.23, f32[512,1024]{1,0:T(8,128)} %collective-permute-done), kind=kOutput, calls=%fused_computation.4 | convolution fusion | flops 3221487616 | bytes 6291456 | tf_op jit(solution)/shard_map/dot_general | solution.py:15
  63.6 0.2 pad_maximum_fusion
  63.8 0.0 copy-start.4
  63.8 47.0 %all_to_all.5 = f32[16,32,1024]{2,1,0:T(8,128)S(1)} all-to-all(f32[16,32,1024]{2,1,0:T(8,128)S(1)} %pad_maximum_fusion), channel_id=1, replica_groups=mesh['blk'=16,'grid'=16] {'grid'}, dimensions={0} | all-to-all | bytes 4194304 | tf_op jit(solution)/shard_map/all_to_all | solution.py:41
  110.9 0.0 copy-done.4
  110.9 1.7 %bitcast_subtract_fusion = f32[1,1,16,32,1024]{4,3,2,1,0:T(8,128)} fusion(f32[1,1,16,32,1024]{4,3,2,1,0:T(8,128)S(1)} %copy-done.4, f32[16,32,1024]{2,1,0:T(8,128)S(1)} %all_to_all.5), kind=kLoop, calls=%fused_computation.3 | loop fusion | flops 524288 | bytes 6291456 | tf_op jit(solution)/shard_map/sub | solution.py:42
  (2 shorter events, 0.0 us)
Async XLA Ops:
  0.0 1.6 %copy-start = (f32[512,1024]{1,0:T(8,128)S(1)}, f32[512,1024]{1,0:T(8,128)}, u32[]{:S(2)}) copy-start(f32[512,1024]{1,0:T(8,128)} %param.7) | copy-start | bytes 6291460
  0.0 53.1 %collective-permute-start = (f32[512,1024]{1,0:T(8,128)}, f32[512,1024]{1,0:T(8,128)}, u32[]{:S(2)}, u32[]{:S(2)}) collective-permute-start(f32[512,1024]{1,0:T(8,128)} %param.5), channel_id=1, source_target_pairs={{0,16},{16,32},{32,48},{48,64},{64,80},{80,96},{96,112},{112,128},... | collective-permute-start | bytes 6291464 | tf_op jit(solution)/shard_map/ppermute | solution.py:11
  7.2 5.9 %copy-start.2 = (f32[16,32,1024]{2,1,0:T(8,128)S(1)}, f32[16,32,1024]{2,1,0:T(8,128)}, u32[]{:S(2)}) copy-start(f32[16,32,1024]{2,1,0:T(8,128)} %gather_fusion.1) | copy-start | bytes 6291460
  7.2 5.9 %copy-start.3 = (f32[512,1024]{1,0:T(8,128)S(1)}, f32[512,1024]{1,0:T(8,128)}, u32[]{:S(2)}) copy-start(f32[512,1024]{1,0:T(8,128)} %param.5) | copy-start | bytes 6291460
  16.7 41.6 %copy-start.1 = (f32[16,32,1024]{2,1,0:T(8,128)S(1)}, f32[16,32,1024]{2,1,0:T(8,128)}, u32[]{:S(2)}) copy-start(f32[16,32,1024]{2,1,0:T(8,128)} %gather_fusion) | copy-start | bytes 6291460
  63.8 47.1 %copy-start.4 = (f32[1,1,16,32,1024]{4,3,2,1,0:T(8,128)S(1)}, f32[1,1,16,32,1024]{4,3,2,1,0:T(8,128)}, u32[]{:S(2)}) copy-start(f32[1,1,16,32,1024]{4,3,2,1,0:T(8,128)} %param.9) | copy-start | bytes 6291460
where the time goes:
time: 113 us
  blocking collectives  47 us (42%)
  waiting for transfers between devices  36.5 us (32%)
  matrix products  19.9 us (18%)
  local copies, waits for them, and re-layouts  6.26 us (6%)
  other arithmetic  2.83 us (3%)
    all_to_all x1, blocking collectives, body(): lax.all_to_all(joined, 'grid', split_axis=0, concat_axis=0, tiled=True)  47 us
    ppermute x1, waiting for transfers between devices, from_behind(): lax.ppermute(array, axis, [(i, (i + by) % length) for i in range(length)])  36.5 us
    dot_general x2, matrix products, hadamard_panel(): jnp.dot(rows_x, panel.T, preferred_element_type=jnp.float32, precision=la...  11.2 us
    dot_general x2, matrix products, hadamard_panel(): jnp.dot(rows_z, panel.T, preferred_element_type=jnp.float32, precision=la...  8.67 us
    gather x1, local copies, waits for them, and re-layouts, body(): times_x.reshape(groups, tile_rows, width)[inverse].reshape(row_count, width)  3.58 us
  transfers between devices with their start and end apart: 1, of which 1 were waited for; matrix products, arithmetic and copies ran while one was open for 14% of the time, Pallas kernels for 0%

commit v1 on v0

v1 whole, which is shorter than its diff:
```python
import jax
import jax.numpy as jnp
from jax import lax
from jax.experimental import pallas as pl
from jax.experimental.pallas import tpu as pltpu
from jax.sharding import PartitionSpec as P

MESH = pl.DeviceIdType.MESH
ROUNDS = 2
PARTS = 4
CUTS = 4


def split(value):
    high = value.astype(jnp.bfloat16)
    return high, (value - high.astype(jnp.float32)).astype(jnp.bfloat16)


def product(left, right):
    return lax.dot_general(
        left, right, (((1,), (1,)), ((), ())), preferred_element_type=jnp.float32
    )


def kernel(
    owner_hbm, c_hbm, x_hbm, z_hbm, out,
    owner, c_own, x_own, z_own, panel, relay, c_high, c_low, lhs_high, lhs_low, send,
    load_sem, panel_send, panel_recv, relay_send, relay_recv, tile_send, tile_recv,
):
    rows, width = c_own.shape
    groups, tile_rows, _ = send.shape
    cut = rows // (PARTS * CUTS)
    blk, grid = lax.axis_index("blk"), lax.axis_index("grid")
    half, y, core = blk // 8, blk // 2 % 4, blk % 2
    x, z = grid // 4, grid % 4

    def at(half_, y_, core_):
        return (half_ * 8 + y_ * 2 + core_, grid)

    behind, ahead = ((blk + 15) % 16, grid), ((blk + 1) % 16, grid)
    other = 1 - half
    target = at(other, 0, 0)
    is_source = jnp.logical_and(core == 1, y == 3)
    is_relay = jnp.logical_and(core == 1, y < 3)
    is_target = jnp.logical_and(core == 0, y == 0)

    loads = [
        pltpu.make_async_copy(far, near, load_sem.at[i])
        for i, (far, near) in enumerate(
            ((c_hbm, c_own), (x_hbm, x_own), (z_hbm, z_own), (owner_hbm, owner))
        )
    ]
    for load in loads:
        load.start()

    barrier = pltpu.get_barrier_semaphore()

    def tell(device):
        pl.semaphore_signal(barrier, inc=1, device_id=device, device_id_type=MESH)

    for step in range(1, groups):
        tell((blk, (grid + step) % groups))
    tell(behind)

    @pl.when(is_target)
    def _():
        for part in range(PARTS - 1):
            tell(at(other, part, 1))

    @pl.when(is_relay)
    def _():
        tell(at(half, 3, 1))

    def to_panel(piece, device):
        at_rows = pl.ds(piece * cut, cut)
        return pltpu.make_async_remote_copy(
            src_ref=c_own.at[at_rows], dst_ref=panel.at[at_rows],
            send_sem=panel_send.at[piece], recv_sem=panel_recv.at[piece],
            device_id=device, device_id_type=MESH,
        )

    def to_relay(part, step):
        piece = part * CUTS + step
        return pltpu.make_async_remote_copy(
            src_ref=c_own.at[pl.ds(piece * cut, cut)], dst_ref=relay.at[step],
            send_sem=panel_send.at[piece], recv_sem=relay_recv.at[step],
            device_id=at(half, part, 1), device_id_type=MESH,
        )

    def from_relay(step):
        piece = y * CUTS + step
        return pltpu.make_async_remote_copy(
            src_ref=relay.at[step], dst_ref=panel.at[pl.ds(piece * cut, cut)],
            send_sem=relay_send.at[step], recv_sem=panel_recv.at[piece],
            device_id=target, device_id_type=MESH,
        )

    def place(j, i):
        flip_1, flip_0 = 1 - j // 2, (j + 1) // 2 % 2
        to_z = 2 * ((z // 2 + flip_1) % 2) + (z % 2 + flip_0) % 2
        return (x + i) % 4 * 4 + to_z

    def to_owner(r, h, source):
        columns = pl.ds(r * rows, rows)
        return pltpu.make_async_remote_copy(
            src_ref=send.at[h, :, columns], dst_ref=out.at[source, :, columns],
            send_sem=tile_send.at[r * groups + h], recv_sem=tile_recv.at[r * groups + source],
            device_id=(blk, h), device_id_type=MESH,
        )

    def gather(j):
        for i in range(4):
            h = place(j, i)
            t = jnp.int32(0)
            for k in range(groups):
                t = jnp.where(owner[k] == h, k, t)
            for k, rows_of in enumerate((x_own, z_own)):
                into = pl.ds((k * 4 + i) * tile_rows, tile_rows)
                high, low = split(rows_of[t])
                lhs_high[into], lhs_low[into] = high, low

    def compute(r, j):
        high, low = lhs_high[...], lhs_low[...]
        count = 4 * tile_rows
        step = 256
        for n in range(rows // step):
            at_rows = slice(n * step, (n + 1) * step)
            both = product(high, c_high[at_rows]) + product(low, c_high[at_rows])
            both = both + product(high, c_low[at_rows])
            block = both[:count] * both[count:]
            for i in range(4):
                send[place(j, i), :, r * rows + n * step : r * rows + (n + 1) * step] = block[
                    i * tile_rows : (i + 1) * tile_rows
                ]

    def ship(r, j):
        for i in range(4):
            copy = to_owner(r, place(j, i), grid)
            if i == 0:
                pl.when(j < 3)(copy.start)
            else:
                copy.start()

    def divide(values):
        for n in range(4):
            at_rows = slice(n * rows // 4, (n + 1) * rows // 4)
            c_high[at_rows], c_low[at_rows] = split(values[at_rows])

    loads[0].wait()
    divide(c_own)
    loads[1].wait()
    loads[2].wait()
    loads[3].wait()
    gather(0)

    @pl.loop(0, 4)
    def _(j):
        compute(0, j)
        gather((j + 1) % 4)

        @pl.when(j == 0)
        def _():
            extra = jnp.where(is_source, PARTS, jnp.where(is_relay, 2, 1))
            pl.semaphore_wait(barrier, groups - 1 + extra)

            @pl.when(jnp.logical_not(is_source))
            def _():
                for piece in range(PARTS * CUTS):
                    to_panel(piece, ahead).start()

            @pl.when(is_source)
            def _():
                for step in range(CUTS):
                    to_panel((PARTS - 1) * CUTS + step, target).start()
                    for part in range(PARTS - 1):
                        to_relay(part, step).start()

        ship(0, j)

    @pl.when(is_relay)
    def _():
        for step in range(CUTS):
            to_relay(0, step).wait_recv()
            from_relay(step).start()

    for piece in range(PARTS * CUTS):
        to_panel(piece, ahead).wait_recv()
    divide(panel)

    @pl.loop(0, 4)
    def _(j):
        compute(1, j)
        gather((j + 1) % 4)
        ship(1, j)

    out[grid] = send[grid]
    for piece in range(PARTS * CUTS):
        to_panel(piece, ahead).wait_send()

    @pl.when(is_relay)
    def _():
        for step in range(CUTS):
            from_relay(step).wait_send()

    for r in range(ROUNDS):

        @pl.loop(1, groups)
        def _(step):
            h = (grid + step) % groups
            copy = to_owner(r, h, h)
            copy.wait_send()
            copy.wait_recv()


def exchange(owner, constraints, times_x, times_zinv):
    rows, width = constraints.shape
    groups = owner.shape[0]
    tile_rows = rows // groups
    pieces = PARTS * CUTS
    word, half = jnp.float32, jnp.bfloat16
    hbm = pl.BlockSpec(memory_space=pltpu.HBM)
    return pl.pallas_call(
        kernel,
        out_shape=jax.ShapeDtypeStruct((groups, tile_rows, ROUNDS * rows), word),
        in_specs=[hbm] * 4,
        out_specs=pl.BlockSpec(memory_space=pltpu.VMEM),
        scratch_shapes=[
            pltpu.SMEM((groups,), jnp.int32),
            pltpu.VMEM((rows, width), word),
            pltpu.VMEM((groups, tile_rows, width), word),
            pltpu.VMEM((groups, tile_rows, width), word),
            pltpu.VMEM((rows, width), word),
            pltpu.VMEM((CUTS, rows // pieces, width), word),
            pltpu.VMEM((rows, width), half),
            pltpu.VMEM((rows, width), half),
            pltpu.VMEM((8 * tile_rows, width), half),
            pltpu.VMEM((8 * tile_rows, width), half),
            pltpu.VMEM((groups, tile_rows, ROUNDS * rows), word),
            pltpu.SemaphoreType.DMA((4,)),
            pltpu.SemaphoreType.DMA((pieces,)),
            pltpu.SemaphoreType.DMA((pieces,)),
            pltpu.SemaphoreType.DMA((CUTS,)),
            pltpu.SemaphoreType.DMA((CUTS,)),
            pltpu.SemaphoreType.DMA((ROUNDS * groups,)),
            pltpu.SemaphoreType.DMA((ROUNDS * groups,)),
        ],
        compiler_params=pltpu.CompilerParams(
            collective_id=0, has_side_effects=True, vmem_limit_bytes=32 << 20
        ),
        name="schur_exchange",
    )(
        *(
            pltpu.with_memory_space_constraint(array, pltpu.HBM)
            for array in (
                owner,
                constraints,
                times_x.reshape(groups, tile_rows, width),
                times_zinv.reshape(groups, tile_rows, width),
            )
        )
    )


def body(constraints, times_x, times_zinv, owner, update):
    joined = exchange(owner[0, 0], constraints, times_x, times_zinv)
    return joined[None, None] - update


def solution(mesh):
    placed = (
        P(("blk", "grid"), None),
        P(("blk", "grid"), None),
        P(("blk", "grid"), None),
        P("blk", "grid", None),
        P("blk", "grid", None, None, None),
    )
    return jax.shard_map(
        body,
        mesh=mesh,
        in_specs=placed,
        out_specs=P("blk", "grid", None, None, None),
        check_vma=False,
    )
```

time: 113 us -> 69 us (0.61)
  the two profiles are of different devices: /device:TPU:128 before, /device:TPU:61 now
where the time goes in v1:
time: 69 us; the launch traced here: 68.1 us
  Pallas kernels  66.2 us (96%)
  other arithmetic  1.88 us (3%)
    pallas_call x1, Pallas kernels, exchange(): pl.pallas_call(kernel, out_shape=jax.ShapeDtypeStruct((groups, tile_rows,...  66.2 us
    sub x1, other arithmetic, body(): return joined[None, None] - update  1.88 us

profile of v1, /device:TPU:61, one launch (start us, length us, event | category | flops | bytes accessed | tf_op | source)
XLA Modules:
  0.0 68.1 jit_solution(7553240866480542576)
XLA Ops:
  0.0 0.0 copy-start
  0.0 66.2 %schur_exchange.1 = f32[16,32,1024]{2,1,0:T(8,128)S(1)} custom-call(s32[16]{0:T(128)} %bitcast.7, f32[512,1024]{1,0:T(8,128)} %c_hbm.1, f32[16,32,1024]{2,1,0:T(8,128)} %bitcast.5, f32[16,32,1024]{2,1,0:T(8,128)} %bitcast.6), custom_call_target="tpu_custom_call" | custom-call | tf_op jit(solution)/shard_map/schur_exchange/pallas_call | solution.py:222
  66.2 0.0 copy-done
  66.2 1.9 %bitcast_subtract_fusion = f32[1,1,16,32,1024]{4,3,2,1,0:T(8,128)} fusion(f32[1,1,16,32,1024]{4,3,2,1,0:T(8,128)S(1)} %copy-done, f32[16,32,1024]{2,1,0:T(8,128)S(1)} %schur_exchange.1), kind=kLoop, calls=%fused_computation | loop fusion | flops 524288 | bytes 6291456 | tf_op jit(solution)/shard_map/sub | solution.py:266
Async XLA Ops:
  0.0 66.2 %copy-start = (f32[1,1,16,32,1024]{4,3,2,1,0:T(8,128)S(1)}, f32[1,1,16,32,1024]{4,3,2,1,0:T(8,128)}, u32[]{:S(2)}) copy-start(f32[1,1,16,32,1024]{4,3,2,1,0:T(8,128)} %param.9) | copy-start | bytes 6291460

commit v2 on v1

--- a/solution.py
+++ b/solution.py
@@ -23,13 +23,14 @@
 
 
 def kernel(
-    owner_hbm, c_hbm, x_hbm, z_hbm, out,
-    owner, c_own, x_own, z_own, panel, relay, c_high, c_low, lhs_high, lhs_low, send,
+    owner_hbm, c_hbm, x_hbm, z_hbm, update_hbm, out,
+    owner, c_own, x_own, z_own, update, panel, relay, c_high, c_low, lhs_high, lhs_low, send,
     load_sem, panel_send, panel_recv, relay_send, relay_recv, tile_send, tile_recv,
 ):
     rows, width = c_own.shape
     groups, tile_rows, _ = send.shape
     cut = rows // (PARTS * CUTS)
+    step_rows = rows // 2
     blk, grid = lax.axis_index("blk"), lax.axis_index("grid")
     half, y, core = blk // 8, blk // 2 % 4, blk % 2
     x, z = grid // 4, grid % 4
@@ -44,13 +45,21 @@
     is_relay = jnp.logical_and(core == 1, y < 3)
     is_target = jnp.logical_and(core == 0, y == 0)
 
+    first, second = pl.ds(0, rows // 2), pl.ds(rows // 2, rows // 2)
     loads = [
         pltpu.make_async_copy(far, near, load_sem.at[i])
         for i, (far, near) in enumerate(
-            ((c_hbm, c_own), (x_hbm, x_own), (z_hbm, z_own), (owner_hbm, owner))
+            (
+                (c_hbm.at[first], c_own.at[first]),
+                (owner_hbm, owner),
+                (x_hbm, x_own),
+                (z_hbm, z_own),
+                (c_hbm.at[second], c_own.at[second]),
+                (update_hbm, update),
+            )
         )
     ]
-    for load in loads:
+    for load in loads[:5]:
         load.start()
 
     barrier = pltpu.get_barrier_semaphore()
@@ -96,12 +105,14 @@
         )
 
     def place(j, i):
-        flip_1, flip_0 = 1 - j // 2, (j + 1) // 2 % 2
+        edge = 1 - (z // 2 + z % 2) % 2
+        flip_1 = (1 - j // 2) * (1 - edge) + edge * ((j + 1) // 2 % 2)
+        flip_0 = (j + 1) // 2 % 2 * (1 - edge) + edge * (1 - j // 2)
         to_z = 2 * ((z // 2 + flip_1) % 2) + (z % 2 + flip_0) % 2
-        return (x + i) % 4 * 4 + to_z
-
-    def to_owner(r, h, source):
-        columns = pl.ds(r * rows, rows)
+        return (0, 1, 3, 2)[i] * 4 + to_z
+
+    def to_owner(r, h, source, start=0, size=None):
+        columns = pl.ds(r * rows + start, size or rows)
         return pltpu.make_async_remote_copy(
             src_ref=send.at[h, :, columns], dst_ref=out.at[source, :, columns],
             send_sem=tile_send.at[r * groups + h], recv_sem=tile_recv.at[r * groups + source],
@@ -119,63 +130,56 @@
                 high, low = split(rows_of[t])
                 lhs_high[into], lhs_low[into] = high, low
 
-    def compute(r, j):
+    def compute(r, j, n):
         high, low = lhs_high[...], lhs_low[...]
         count = 4 * tile_rows
-        step = 256
-        for n in range(rows // step):
-            at_rows = slice(n * step, (n + 1) * step)
-            both = product(high, c_high[at_rows]) + product(low, c_high[at_rows])
-            both = both + product(high, c_low[at_rows])
-            block = both[:count] * both[count:]
-            for i in range(4):
-                send[place(j, i), :, r * rows + n * step : r * rows + (n + 1) * step] = block[
-                    i * tile_rows : (i + 1) * tile_rows
-                ]
-
-    def ship(r, j):
+        at_rows = slice(n * step_rows, (n + 1) * step_rows)
+        both = product(high, c_high[at_rows]) + product(low, c_high[at_rows])
+        both = both + product(high, c_low[at_rows])
+        block = both[:count] * both[count:]
+        columns = slice(r * rows + n * step_rows, r * rows + (n + 1) * step_rows)
         for i in range(4):
-            copy = to_owner(r, place(j, i), grid)
-            if i == 0:
-                pl.when(j < 3)(copy.start)
-            else:
-                copy.start()
-
-    def divide(values):
-        for n in range(4):
-            at_rows = slice(n * rows // 4, (n + 1) * rows // 4)
+            send[place(j, i), :, columns] = block[i * tile_rows : (i + 1) * tile_rows]
+
+    def ship(r, j, start=0, size=None):
+        for i in range(4):
+            copy = to_owner(r, place(j, i), grid, start, size)
+            pl.when(place(j, i) != grid)(copy.start)
+
+    def divide(values, start, stop):
+        for n in range(start, stop, 128):
+            at_rows = slice(n, n + 128)
             c_high[at_rows], c_low[at_rows] = split(values[at_rows])
 
     loads[0].wait()
-    divide(c_own)
-    loads[1].wait()
-    loads[2].wait()
-    loads[3].wait()
+    divide(c_own, 0, rows // 2)
+    for load in loads[1:4]:
+        load.wait()
     gather(0)
-
-    @pl.loop(0, 4)
-    def _(j):
-        compute(0, j)
-        gather((j + 1) % 4)
-
-        @pl.when(j == 0)
-        def _():
-            extra = jnp.where(is_source, PARTS, jnp.where(is_relay, 2, 1))
-            pl.semaphore_wait(barrier, groups - 1 + extra)
-
-            @pl.when(jnp.logical_not(is_source))
-            def _():
-                for piece in range(PARTS * CUTS):
-                    to_panel(piece, ahead).start()
-
-            @pl.when(is_source)
-            def _():
-                for step in range(CUTS):
-                    to_panel((PARTS - 1) * CUTS + step, target).start()
-                    for part in range(PARTS - 1):
-                        to_relay(part, step).start()
-
-        ship(0, j)
+    start = jnp.int32(0)
+    compute(0, start, 0)
+    loads[4].wait()
+    extra = jnp.where(is_source, PARTS, jnp.where(is_relay, 2, 1))
+    pl.semaphore_wait(barrier, groups - 1 + extra)
+
+    @pl.when(jnp.logical_not(is_source))
+    def _():
+        for piece in range(PARTS * CUTS):
+            to_panel(piece, ahead).start()
+
+    @pl.when(is_source)
+    def _():
+        for step in range(CUTS):
+            to_panel((PARTS - 1) * CUTS + step, target).start()
+            for part in range(PARTS - 1):
+                to_relay(part, step).start()
+
+    ship(0, start, 0, step_rows)
+    divide(c_own, rows // 2, rows)
+    compute(0, start, 1)
+    gather(1)
+    ship(0, start, step_rows, rows - step_rows)
+    loads[5].start()
 
     @pl.when(is_relay)
     def _():
@@ -183,17 +187,35 @@
             to_relay(0, step).wait_recv()
             from_relay(step).start()
 
+    @pl.loop(1, 4)
+    def _(j):
+        for n in range(rows // step_rows):
+            compute(0, j, n)
+        gather((j + 1) % 4)
+        ship(0, j)
+
     for piece in range(PARTS * CUTS):
         to_panel(piece, ahead).wait_recv()
-    divide(panel)
+    divide(panel, 0, rows)
 
     @pl.loop(0, 4)
     def _(j):
-        compute(1, j)
+        for n in range(rows // step_rows):
+            compute(1, j, n)
         gather((j + 1) % 4)
         ship(1, j)
 
-    out[grid] = send[grid]
+    loads[5].wait()
+    out[grid] = send[grid] - update[grid]
+    for r in range(ROUNDS):
+
+        @pl.loop(0, groups - 1)
+        def _(step):
+            h = (grid + step + 1) % groups
+            columns = slice(r * rows, (r + 1) * rows)
+            to_owner(r, h, h).wait_recv()
+            out[h, :, columns] = out[h, :, columns] - update[h, :, columns]
+
     for piece in range(PARTS * CUTS):
         to_panel(piece, ahead).wait_send()
 
@@ -207,12 +229,10 @@
         @pl.loop(1, groups)
         def _(step):
             h = (grid + step) % groups
-            copy = to_owner(r, h, h)
-            copy.wait_send()
-            copy.wait_recv()
-
-
-def exchange(owner, constraints, times_x, times_zinv):
+            to_owner(r, h, h).wait_send()
+
+
+def exchange(owner, constraints, times_x, times_zinv, update):
     rows, width = constraints.shape
     groups = owner.shape[0]
     tile_rows = rows // groups
@@ -222,13 +242,14 @@
     return pl.pallas_call(
         kernel,
         out_shape=jax.ShapeDtypeStruct((groups, tile_rows, ROUNDS * rows), word),
-        in_specs=[hbm] * 4,
+        in_specs=[hbm] * 5,
         out_specs=pl.BlockSpec(memory_space=pltpu.VMEM),
         scratch_shapes=[
             pltpu.SMEM((groups,), jnp.int32),
             pltpu.VMEM((rows, width), word),
             pltpu.VMEM((groups, tile_rows, width), word),
             pltpu.VMEM((groups, tile_rows, width), word),
+            pltpu.VMEM((groups, tile_rows, ROUNDS * rows), word),
             pltpu.VMEM((rows, width), word),
             pltpu.VMEM((CUTS, rows // pieces, width), word),
             pltpu.VMEM((rows, width), half),
@@ -236,7 +257,7 @@
             pltpu.VMEM((8 * tile_rows, width), half),
             pltpu.VMEM((8 * tile_rows, width), half),
             pltpu.VMEM((groups, tile_rows, ROUNDS * rows), word),
-            pltpu.SemaphoreType.DMA((4,)),
+            pltpu.SemaphoreType.DMA((6,)),
             pltpu.SemaphoreType.DMA((pieces,)),
             pltpu.SemaphoreType.DMA((pieces,)),
             pltpu.SemaphoreType.DMA((CUTS,)),
@@ -256,14 +277,14 @@
                 constraints,
                 times_x.reshape(groups, tile_rows, width),
                 times_zinv.reshape(groups, tile_rows, width),
+                update,
             )
         )
     )
 
 
 def body(constraints, times_x, times_zinv, owner, update):
-    joined = exchange(owner[0, 0], constraints, times_x, times_zinv)
-    return joined[None, None] - update
+    return exchange(owner[0, 0], constraints, times_x, times_zinv, update[0, 0])[None, None]
 
 
 def solution(mesh):

time: 69 us -> 67.5 us (0.978); the launches traced: 68.1 us -> 67.4 us
  other arithmetic: 1.88 us -> 0 us
  local copies, waits for them, and re-layouts: 0.01 us -> 1.32 us
    sub x1 -> x0, other arithmetic: 1.88 us -> none  [body(): return joined[None, None] - update]
    unnamed x2 -> x1, local copies, waits for them, and re-layouts: 0.01 us -> 1.32 us
where the time goes in v2:
time: 67.5 us; the launch traced here: 67.4 us
  Pallas kernels  66.1 us (98%)
  local copies, waits for them, and re-layouts  1.32 us (2%)
    pallas_call x1, Pallas kernels, exchange(): pl.pallas_call(kernel, out_shape=jax.ShapeDtypeStruct((groups, tile_rows,...  66.1 us

profile of v2, /device:TPU:61, one launch (start us, length us, event | category | flops | bytes accessed | tf_op | source)
XLA Modules:
  0.0 67.4 jit_solution(12526931648490296829)
XLA Ops:
  0.0 66.1 %schur_exchange.1 = f32[16,32,1024]{2,1,0:T(8,128)S(1)} custom-call(s32[16]{0:T(128)} %bitcast.9, f32[512,1024]{1,0:T(8,128)} %c_hbm.1, f32[16,32,1024]{2,1,0:T(8,128)} %bitcast.6, f32[16,32,1024]{2,1,0:T(8,128)} %bitcast.7, f32[16,32,1024]{2,1,0:T(8,128)} %bitcast.8), custom_call_target="tpu_custom_call" | custom-call | tf_op jit(solution)/shard_map/schur_exchange/pallas_call | solution.py:242
  66.1 1.3 %copy.7 = f32[1,1,16,32,1024]{4,3,2,1,0:T(8,128)} copy(f32[1,1,16,32,1024]{4,3,2,1,0:T(8,128)S(1)} %bitcast.5) | data formatting | bytes 4194304

commit v3 on v2

--- a/solution.py
+++ b/solution.py
@@ -25,12 +25,14 @@
 def kernel(
     owner_hbm, c_hbm, x_hbm, z_hbm, update_hbm, out,
     owner, c_own, x_own, z_own, update, panel, relay, c_high, c_low, lhs_high, lhs_low, send,
-    load_sem, panel_send, panel_recv, relay_send, relay_recv, tile_send, tile_recv,
+    turn, load_sem, panel_send, panel_recv, relay_send, relay_recv, turn_send, turn_recv,
+    tile_send, tile_recv,
 ):
     rows, width = c_own.shape
     groups, tile_rows, _ = send.shape
     cut = rows // (PARTS * CUTS)
     step_rows = rows // 2
+    turn_rows = turn.shape[0]
     blk, grid = lax.axis_index("blk"), lax.axis_index("grid")
     half, y, core = blk // 8, blk // 2 % 4, blk % 2
     x, z = grid // 4, grid % 4
@@ -44,6 +46,42 @@
     is_source = jnp.logical_and(core == 1, y == 3)
     is_relay = jnp.logical_and(core == 1, y < 3)
     is_target = jnp.logical_and(core == 0, y == 0)
+    edge = 1 - (z // 2 + z % 2) % 2
+    is_turn = jnp.logical_and(core == 1, edge == 1)
+    turned_z = (1 - half) * (1 + z // 3) + half * (3 - z)
+    turn_source = (7, x * 4 + turned_z)
+    turn_target = (8, x * 4 + turned_z)
+
+    def turn_at(part):
+        return (edge * 8 + part * 2 + 1, x * 4 + 3 * (1 - z % 2))
+
+
+    barrier = pltpu.get_barrier_semaphore()
+
+    def tell(device):
+        pl.semaphore_signal(barrier, inc=1, device_id=device, device_id_type=MESH)
+
+    for step in range(1, groups):
+        tell((blk, (grid + step) % groups))
+    tell(behind)
+
+    @pl.when(is_target)
+    def _():
+        for part in range(PARTS - 1):
+            tell(at(other, part, 1))
+
+    @pl.when(is_relay)
+    def _():
+        tell(at(half, 3, 1))
+
+    @pl.when(is_turn)
+    def _():
+        tell(turn_source)
+
+    @pl.when(jnp.logical_and(is_target, half == 1))
+    def _():
+        for part in range(PARTS):
+            tell(turn_at(part))
 
     first, second = pl.ds(0, rows // 2), pl.ds(rows // 2, rows // 2)
     loads = [
@@ -62,54 +100,52 @@
     for load in loads[:5]:
         load.start()
 
-    barrier = pltpu.get_barrier_semaphore()
-
-    def tell(device):
-        pl.semaphore_signal(barrier, inc=1, device_id=device, device_id_type=MESH)
-
-    for step in range(1, groups):
-        tell((blk, (grid + step) % groups))
-    tell(behind)
-
-    @pl.when(is_target)
-    def _():
-        for part in range(PARTS - 1):
-            tell(at(other, part, 1))
-
-    @pl.when(is_relay)
-    def _():
-        tell(at(half, 3, 1))
-
-    def to_panel(piece, device):
-        at_rows = pl.ds(piece * cut, cut)
+    def to_panel(piece, device, skip=0):
+        at_rows = pl.ds(piece * cut + skip, cut - skip)
         return pltpu.make_async_remote_copy(
             src_ref=c_own.at[at_rows], dst_ref=panel.at[at_rows],
             send_sem=panel_send.at[piece], recv_sem=panel_recv.at[piece],
             device_id=device, device_id_type=MESH,
         )
 
-    def to_relay(part, step):
+    def to_relay(part, step, skip=0):
         piece = part * CUTS + step
         return pltpu.make_async_remote_copy(
-            src_ref=c_own.at[pl.ds(piece * cut, cut)], dst_ref=relay.at[step],
+            src_ref=c_own.at[pl.ds(piece * cut + skip, cut - skip)],
+            dst_ref=relay.at[step, pl.ds(skip, cut - skip)],
             send_sem=panel_send.at[piece], recv_sem=relay_recv.at[step],
             device_id=at(half, part, 1), device_id_type=MESH,
         )
 
-    def from_relay(step):
+    def to_turn(part):
+        return pltpu.make_async_remote_copy(
+            src_ref=c_own.at[pl.ds(part * CUTS * cut, turn_rows)], dst_ref=turn,
+            send_sem=panel_send.at[part * CUTS], recv_sem=turn_recv.at[0],
+            device_id=turn_at(part), device_id_type=MESH,
+        )
+
+    def from_turn():
+        piece = y * CUTS
+        return pltpu.make_async_remote_copy(
+            src_ref=turn, dst_ref=panel.at[pl.ds(piece * cut, turn_rows)],
+            send_sem=turn_send.at[0], recv_sem=panel_recv.at[piece],
+            device_id=turn_target, device_id_type=MESH,
+        )
+
+    def from_relay(step, skip=0):
         piece = y * CUTS + step
         return pltpu.make_async_remote_copy(
-            src_ref=relay.at[step], dst_ref=panel.at[pl.ds(piece * cut, cut)],
+            src_ref=relay.at[step, pl.ds(skip, cut - skip)],
+            dst_ref=panel.at[pl.ds(piece * cut + skip, cut - skip)],
             send_sem=relay_send.at[step], recv_sem=panel_recv.at[piece],
             device_id=target, device_id_type=MESH,
         )
 
     def place(j, i):
-        edge = 1 - (z // 2 + z % 2) % 2
         flip_1 = (1 - j // 2) * (1 - edge) + edge * ((j + 1) // 2 % 2)
         flip_0 = (j + 1) // 2 % 2 * (1 - edge) + edge * (1 - j // 2)
         to_z = 2 * ((z // 2 + flip_1) % 2) + (z % 2 + flip_0) % 2
-        return (0, 1, 3, 2)[i] * 4 + to_z
+        return ((x + (2, 1, 3, 0)[i]) % 4) * 4 + to_z
 
     def to_owner(r, h, source, start=0, size=None):
         columns = pl.ds(r * rows + start, size or rows)
@@ -160,6 +196,8 @@
     compute(0, start, 0)
     loads[4].wait()
     extra = jnp.where(is_source, PARTS, jnp.where(is_relay, 2, 1))
+    extra = extra + jnp.where(jnp.logical_and(is_source, half == 0), PARTS, 0)
+    extra = extra + jnp.where(is_turn, 1, 0)
     pl.semaphore_wait(barrier, groups - 1 + extra)
 
     @pl.when(jnp.logical_not(is_source))
@@ -169,7 +207,22 @@
 
     @pl.when(is_source)
     def _():
-        for step in range(CUTS):
+        def start_first(skip):
+            to_panel((PARTS - 1) * CUTS, target, skip).start()
+            for part in range(PARTS - 1):
+                to_relay(part, 0, skip).start()
+
+        @pl.when(half == 0)
+        def _():
+            for part in range(PARTS):
+                to_turn(part).start()
+            start_first(turn_rows)
+
+        @pl.when(half == 1)
+        def _():
+            start_first(0)
+
+        for step in range(1, CUTS):
             to_panel((PARTS - 1) * CUTS + step, target).start()
             for part in range(PARTS - 1):
                 to_relay(part, step).start()
@@ -183,9 +236,26 @@
 
     @pl.when(is_relay)
     def _():
-        for step in range(CUTS):
+        def forward_first(skip):
+            to_relay(0, 0, skip).wait_recv()
+            from_relay(0, skip).start()
+
+        @pl.when(half == 0)
+        def _():
+            forward_first(turn_rows)
+
+        @pl.when(half == 1)
+        def _():
+            forward_first(0)
+
+        for step in range(1, CUTS):
             to_relay(0, step).wait_recv()
             from_relay(step).start()
+
+    @pl.when(is_turn)
+    def _():
+        to_turn(0).wait_recv()
+        from_turn().start()
 
     @pl.loop(1, 4)
     def _(j):
@@ -221,8 +291,12 @@
 
     @pl.when(is_relay)
     def _():
-        for step in range(CUTS):
+        pl.when(half == 0)(from_relay(0, turn_rows).wait_send)
+        pl.when(half == 1)(from_relay(0).wait_send)
+        for step in range(1, CUTS):
             from_relay(step).wait_send()
+
+    pl.when(is_turn)(from_turn().wait_send)
 
     for r in range(ROUNDS):
 
@@ -257,11 +331,14 @@
             pltpu.VMEM((8 * tile_rows, width), half),
             pltpu.VMEM((8 * tile_rows, width), half),
             pltpu.VMEM((groups, tile_rows, ROUNDS * rows), word),
+            pltpu.VMEM((rows // pieces // 2, width), word),
             pltpu.SemaphoreType.DMA((6,)),
             pltpu.SemaphoreType.DMA((pieces,)),
             pltpu.SemaphoreType.DMA((pieces,)),
             pltpu.SemaphoreType.DMA((CUTS,)),
             pltpu.SemaphoreType.DMA((CUTS,)),
+            pltpu.SemaphoreType.DMA((1,)),
+            pltpu.SemaphoreType.DMA((1,)),
             pltpu.SemaphoreType.DMA((ROUNDS * groups,)),
             pltpu.SemaphoreType.DMA((ROUNDS * groups,)),
         ],

time: 67.5 us -> 66.7 us (0.988); the launches traced: 67.4 us -> 65.9 us
  Pallas kernels: 66.1 us -> 64.5 us
    pallas_call x1, Pallas kernels: 66.1 us -> 64.5 us  [exchange(): pl.pallas_call(kernel, out_shape=jax.ShapeDtypeStruct((groups, tile_rows,...]
where the time goes in v3:
time: 66.7 us; the launch traced here: 65.9 us
  Pallas kernels  64.5 us (97%)
  local copies, waits for them, and re-layouts  1.32 us (2%)
    pallas_call x1, Pallas kernels, exchange(): pl.pallas_call(kernel, out_shape=jax.ShapeDtypeStruct((groups, tile_rows,...  64.5 us

profile of v3, /device:TPU:61, one launch (start us, length us, event | category | flops | bytes accessed | tf_op | source)
XLA Modules:
  0.0 65.9 jit_solution(17799366428018856841)
XLA Ops:
  0.0 64.5 %schur_exchange.1 = f32[16,32,1024]{2,1,0:T(8,128)S(1)} custom-call(s32[16]{0:T(128)} %bitcast.9, f32[512,1024]{1,0:T(8,128)} %c_hbm.1, f32[16,32,1024]{2,1,0:T(8,128)} %bitcast.6, f32[16,32,1024]{2,1,0:T(8,128)} %bitcast.7, f32[16,32,1024]{2,1,0:T(8,128)} %bitcast.8), custom_call_target="tpu_custom_call" | custom-call | tf_op jit(solution)/shard_map/schur_exchange/pallas_call | solution.py:316
  64.5 1.3 %copy.7 = f32[1,1,16,32,1024]{4,3,2,1,0:T(8,128)} copy(f32[1,1,16,32,1024]{4,3,2,1,0:T(8,128)S(1)} %bitcast.5) | data formatting | bytes 4194304

commit v4 on v3

--- a/solution.py
+++ b/solution.py
@@ -272,20 +272,11 @@
     def _(j):
         for n in range(rows // step_rows):
             compute(1, j, n)
-        gather((j + 1) % 4)
+        pl.when(j < 3)(lambda: gather(j + 1))
         ship(1, j)
 
     loads[5].wait()
     out[grid] = send[grid] - update[grid]
-    for r in range(ROUNDS):
-
-        @pl.loop(0, groups - 1)
-        def _(step):
-            h = (grid + step + 1) % groups
-            columns = slice(r * rows, (r + 1) * rows)
-            to_owner(r, h, h).wait_recv()
-            out[h, :, columns] = out[h, :, columns] - update[h, :, columns]
-
     for piece in range(PARTS * CUTS):
         to_panel(piece, ahead).wait_send()
 
@@ -304,6 +295,18 @@
         def _(step):
             h = (grid + step) % groups
             to_owner(r, h, h).wait_send()
+
+        @pl.loop(0, groups)
+        def _(step):
+            m = step // 4
+            from_z = 2 * ((z // 2 + m // 2) % 2) + (z % 2 + (m + 1) // 2 % 2) % 2
+            h = (x + step) % 4 * 4 + from_z
+            columns = slice(r * rows, (r + 1) * rows)
+
+            @pl.when(h != grid)
+            def _():
+                to_owner(r, h, h).wait_recv()
+                out[h, :, columns] = out[h, :, columns] - update[h, :, columns]
 
 
 def exchange(owner, constraints, times_x, times_zinv, update):

time: 66.7 us -> 66.5 us (level)
  no operation moved by 1% of the time
where the time goes in v4:
time: 66.5 us; the launch traced here: 65.4 us
  Pallas kernels  64.1 us (96%)
  local copies, waits for them, and re-layouts  1.32 us (2%)
    pallas_call x1, Pallas kernels, exchange(): pl.pallas_call(kernel, out_shape=jax.ShapeDtypeStruct((groups, tile_rows,...  64.1 us

profile of v4, /device:TPU:61, one launch (start us, length us, event | category | flops | bytes accessed | tf_op | source)
XLA Modules:
  0.0 65.4 jit_solution(2783909354445097302)
XLA Ops:
  0.0 64.1 %schur_exchange.1 = f32[16,32,1024]{2,1,0:T(8,128)S(1)} custom-call(s32[16]{0:T(128)} %bitcast.9, f32[512,1024]{1,0:T(8,128)} %c_hbm.1, f32[16,32,1024]{2,1,0:T(8,128)} %bitcast.6, f32[16,32,1024]{2,1,0:T(8,128)} %bitcast.7, f32[16,32,1024]{2,1,0:T(8,128)} %bitcast.8), custom_call_target="tpu_custom_call" | custom-call | tf_op jit(solution)/shard_map/schur_exchange/pallas_call | solution.py:319
  64.1 1.3 %copy.7 = f32[1,1,16,32,1024]{4,3,2,1,0:T(8,128)} copy(f32[1,1,16,32,1024]{4,3,2,1,0:T(8,128)S(1)} %bitcast.5) | data formatting | bytes 4194304

commit v5 on v4

--- a/solution.py
+++ b/solution.py
@@ -200,6 +200,8 @@
     extra = extra + jnp.where(is_turn, 1, 0)
     pl.semaphore_wait(barrier, groups - 1 + extra)
 
+    ship(0, start, 0, step_rows)
+
     @pl.when(jnp.logical_not(is_source))
     def _():
         for piece in range(PARTS * CUTS):
@@ -227,7 +229,6 @@
             for part in range(PARTS - 1):
                 to_relay(part, step).start()
 
-    ship(0, start, 0, step_rows)
     divide(c_own, rows // 2, rows)
     compute(0, start, 1)
     gather(1)

time: 66.5 us -> 66.5 us (level)
  no operation moved by 1% of the time
where the time goes in v5:
time: 66.5 us; the launch traced here: 65.4 us
  Pallas kernels  64 us (96%)
  local copies, waits for them, and re-layouts  1.32 us (2%)
    pallas_call x1, Pallas kernels, exchange(): pl.pallas_call(kernel, out_shape=jax.ShapeDtypeStruct((groups, tile_rows,...  64 us

profile of v5, /device:TPU:61, one launch (start us, length us, event | category | flops | bytes accessed | tf_op | source)
XLA Modules:
  0.0 65.4 jit_solution(12484597857246701962)
XLA Ops:
  0.0 64.0 %schur_exchange.1 = f32[16,32,1024]{2,1,0:T(8,128)S(1)} custom-call(s32[16]{0:T(128)} %bitcast.9, f32[512,1024]{1,0:T(8,128)} %c_hbm.1, f32[16,32,1024]{2,1,0:T(8,128)} %bitcast.6, f32[16,32,1024]{2,1,0:T(8,128)} %bitcast.7, f32[16,32,1024]{2,1,0:T(8,128)} %bitcast.8), custom_call_target="tpu_custom_call" | custom-call | tf_op jit(solution)/shard_map/schur_exchange/pallas_call | solution.py:320
  64.1 1.3 %copy.7 = f32[1,1,16,32,1024]{4,3,2,1,0:T(8,128)} copy(f32[1,1,16,32,1024]{4,3,2,1,0:T(8,128)S(1)} %bitcast.5) | data formatting | bytes 4194304
